TPU v7x, 1024 devices: a whole 4x8x16 slice. The times are simulated.
1024 devices in a mesh: gx: 32 (over z_hi, y), gy: 32 (over x, z_lo, core).
Axes of the slice: x: 4, y: 8, z: 16 (z_hi: 4, z_lo: 4; z = z_hi * 4 + z_lo), core: 2. Of those that a mesh axis runs over, the one named last changes fastest.
Arguments:
- checkpoint: float32 [16, 256, 4096], P(None, 'gy', 'gx'), may hold values from -6 to 6
- trajectory: float32 [16, 256, 4096], P(None, 'gy', 'gx'), may hold values from -6 to 6
- adjoint_forcing: float32 [16, 256, 4096], P(None, 'gy', 'gx'), may hold values from -6 to 6
- east_diffusion: float32 [16, 256, 4096], P(None, 'gy', 'gx'), may hold values from 0.1 to 1
- north_diffusion: float32 [16, 256, 4096], P(None, 'gy', 'gx'), may hold values from 0.3 to 3
- east_wind: float32 [16, 256, 4096], P(None, 'gy', 'gx'), may hold values from -0.6 to 0.6
- north_wind: float32 [16, 256, 4096], P(None, 'gy', 'gx'), may hold values from -6 to 6, as said below
- level_diffusion: float32 [16], replicated, may hold values from 0.1 to 1
- damping: float32 [16], replicated, may hold values from 0.2 to 2
- source: float32 [16, 256, 4096], P(None, 'gy', 'gx'), may hold values from -4 to 5
- observations: float32 [16, 256, 4096], P(None, 'gy', 'gx'), may hold values from -6 to 6
- observation_weight: float32 [16, 256, 4096], P(None, 'gy', 'gx'), may hold values from 0.1 to 1
- step_index: int32 [1], replicated, may hold values from 0 to 95
Outputs:
- forward_state: float32 [16, 256, 4096], P(None, 'gy', 'gx')
- forward_residual: float32 [16, 256, 4096], P(None, 'gy', 'gx')
- adjoint_state: float32 [16, 256, 4096], P(None, 'gy', 'gx')
Inputs may be any that keep to these rules, and one draw needn't show every extreme that they name: At every face the magnitude of north_wind is at most twice north_diffusion.
All inputs are finite; a program needn't handle non-finite values.
Results may differ from a plain program's by a relative error of at most 0.000091.
Values sent between devices are 32-bit elements; how exact they have to be, the bound alone decides.
No kernel may reach another device: no remote copies, remote signals or barrier semaphores. Data moves between devices by JAX's collectives and lax.ppermute only.
A program may use at most 32 MiB of HBM per device.

v0:
```python
import math

import jax
import jax.numpy as jnp
from jax import lax
from jax.sharding import PartitionSpec as P

OUTER = 2
INNER = 4
DAY_STEPS = 96


RELAXATION = 0.7


def extended(block, sides, width, periodic):
    for axis, dim in sides:
        count = lax.axis_size(axis)
        forward = [(i, i + 1) for i in range(count - 1)]
        if periodic:
            forward.append((count - 1, 0))
        backward = [(target, source) for source, target in forward]
        low = lax.ppermute(
            lax.slice_in_dim(block, block.shape[dim] - width, None, axis=dim), axis, forward
        )
        high = lax.ppermute(lax.slice_in_dim(block, 0, width, axis=dim), axis, backward)
        block = jnp.concatenate([low, block, high], axis=dim)
    return block


def shifted(array, axis, by):
    size = lax.axis_size(axis)
    return lax.ppermute(array, axis, [(i, (i + by) % size) for i in range(size)])


def shifted_2(block, axis, distance):
    devices = range(lax.axis_size(axis))
    route = [(i - distance, i) for i in devices if i - distance in devices]
    return lax.ppermute(block, axis, route)


def vertical_part(field, up_coef):
    zero_level = jnp.zeros_like(field[:1])
    padded = jnp.concatenate([zero_level, field, zero_level], axis=0)
    flux = up_coef[:, None, None] * (padded[1:] - padded[:-1])
    return -(flux[1:] - flux[:-1])


def apply_forward(west_east, south_north, field, faces):
    east_coef, east_flow, north_coef, north_flow, up_coef = faces
    flux_east = east_flow * (west_east[..., 1:] + west_east[..., :-1]) * 0.5 - east_coef * (
        west_east[..., 1:] - west_east[..., :-1]
    )
    flux_north = north_flow * (south_north[:, 1:] + south_north[:, :-1]) * 0.5 - north_coef * (
        south_north[:, 1:] - south_north[:, :-1]
    )
    return (
        flux_east[..., 1:]
        - flux_east[..., :-1]
        + (flux_north[:, 1:] - flux_north[:, :-1])
        + vertical_part(field, up_coef)
    )


def scatter_parts(field, faces):
    east_coef, east_flow, north_coef, north_flow, up_coef = faces
    padded_east = jnp.pad(field, ((0, 0), (0, 0), (1, 1)))
    weight_east = padded_east[..., :-1] - padded_east[..., 1:]
    spread_east = jnp.pad(weight_east * (east_flow * 0.5 + east_coef), ((0, 0), (0, 0), (0, 1)))
    spread_east = spread_east + jnp.pad(
        weight_east * (east_flow * 0.5 - east_coef), ((0, 0), (0, 0), (1, 0))
    )
    padded_north = jnp.pad(field, ((0, 0), (1, 1), (0, 0)))
    weight_north = padded_north[:, :-1] - padded_north[:, 1:]
    spread_north = jnp.pad(weight_north * (north_flow * 0.5 + north_coef), ((0, 0), (0, 1), (0, 0)))
    spread_north = spread_north + jnp.pad(
        weight_north * (north_flow * 0.5 - north_coef), ((0, 0), (1, 0), (0, 0))
    )
    middle = spread_east[..., 1:-1] + spread_north[:, 1:-1] + vertical_part(field, up_coef)
    blank_east = jnp.zeros_like(field[..., 2:])
    rim_east = jnp.concatenate([spread_east[..., :1], blank_east, spread_east[..., -1:]], axis=2)
    blank_north = jnp.zeros_like(field[:, 2:])
    rim_north = jnp.concatenate([spread_north[:, :1], blank_north, spread_north[:, -1:]], axis=1)
    return (middle, rim_east, rim_north)


def scatter_finish(middle, west_east, south_north):
    blank_east = jnp.zeros_like(middle[..., 2:])
    arrived_east = jnp.concatenate([west_east[..., :1], blank_east, west_east[..., -1:]], axis=2)
    blank_north = jnp.zeros_like(middle[:, 2:])
    arrived_north = jnp.concatenate([south_north[:, :1], blank_north, south_north[:, -1:]], axis=1)
    return middle + arrived_east + arrived_north


def diagonal_of(tangent, faces, damping):
    east_coef, east_flow, north_coef, north_flow, up_coef = faces
    total = 1.0 + east_coef[..., 1:] + east_coef[..., :-1] + north_coef[:, 1:] + north_coef[:, :-1]
    total = total + (up_coef[1:] + up_coef[:-1])[:, None, None]
    return total + damping[:, None, None] * (1.0 - tangent * tangent)


def lon_extend(stacked):
    return extended(stacked, (("gx", 3),), 1, True)


def lat_extend(stacked):
    return extended(stacked, (("gy", 2),), 1, False)


def run_tasks(tasks):
    west_east = lon_extend(jnp.stack([pending[0] for pending in tasks]))
    south_north = lat_extend(jnp.stack([pending[1] for pending in tasks]))
    return [
        pending[2](west_east[number], south_north[number]) for number, pending in enumerate(tasks)
    ]


def per_device(
    checkpoint,
    trajectory,
    adjoint_forcing,
    east_diffusion,
    north_diffusion,
    east_wind,
    north_wind,
    level_diffusion,
    damping,
    source,
    observations,
    observation_weight,
    step_index,
):
    levels, lat_rows, lon_cols = checkpoint.shape
    row_global = lax.axis_index("gy") * lat_rows + jnp.arange(lat_rows, dtype=jnp.int32)
    row_mask = (row_global < lat_rows * lax.axis_size("gy") - 1).astype(jnp.float32)[None, :, None]
    level_mask = (jnp.arange(levels) < levels - 1).astype(jnp.float32)
    north_masked = north_diffusion * row_mask
    flow_masked = north_wind * row_mask
    up_coef = jnp.concatenate([jnp.zeros_like(level_diffusion[:1]), level_diffusion * level_mask])
    column = (lax.axis_index("gx") * lon_cols + jnp.arange(lon_cols, dtype=jnp.int32)).astype(
        jnp.float32
    )
    phase = (
        2.0 * math.pi * column / (lon_cols * lax.axis_size("gx"))
        - 2.0 * math.pi * step_index[0].astype(jnp.float32) / DAY_STEPS
    )
    forcing = source * jnp.cos(phase)[None, None, :]
    damp = damping[:, None, None]
    edge_west = shifted(jnp.stack([east_diffusion[..., -1:], east_wind[..., -1:]]), "gx", 1)
    edge_south = shifted_2(jnp.stack([north_masked[:, -1:], flow_masked[:, -1:]]), "gy", 1)
    faces = (
        jnp.concatenate([edge_west[0], east_diffusion], axis=2),
        jnp.concatenate([edge_west[1], east_wind], axis=2),
        jnp.concatenate([edge_south[0], north_masked], axis=1),
        jnp.concatenate([edge_south[1], flow_masked], axis=1),
        up_coef,
    )

    def forward_task(field):
        return (
            field,
            field,
            lambda west_east, south_north: apply_forward(west_east, south_north, field, faces),
        )

    def adjoint_task(field):
        middle, rim_east, rim_north = scatter_parts(field, faces)
        return (
            rim_east,
            rim_north,
            lambda west_east, south_north: scatter_finish(middle, west_east, south_north),
        )

    forward = {"state": checkpoint}

    def forward_update(section, closing, applied):
        if section == "res":
            state = forward["state"]
            tangent = jnp.tanh(state)
            diagonal = diagonal_of(tangent, faces, damping)
            resid = state - checkpoint + applied + damp * tangent - forcing
            forward["tangent"] = tangent
            forward["diagonal"] = diagonal
            forward["resid"] = resid
            forward["delta"] = -RELAXATION * resid / diagonal
        elif section == "lin":
            tangent = forward["tangent"]
            delta = forward["delta"]
            image = delta + applied + damp * (1.0 - tangent * tangent) * delta
            forward["delta"] = (
                delta + RELAXATION * (-forward["resid"] - image) / forward["diagonal"]
            )
        else:
            state = forward["state"]
            forward["final"] = state - checkpoint + applied + damp * jnp.tanh(state) - forcing
        if closing:
            forward["state"] = forward["state"] + forward["delta"]

    tangent_n = jnp.tanh(trajectory)
    diagonal_n = diagonal_of(tangent_n, faces, damping)
    local_n = damp * (1.0 - tangent_n * tangent_n)
    start_resid = -adjoint_forcing
    adjoint = {
        "mult": jnp.zeros_like(trajectory),
        "resid": start_resid,
        "delta": -RELAXATION * start_resid / diagonal_n,
    }

    def adjoint_update(section, closing, applied):
        if section == "res":
            multiplier = adjoint["mult"]
            resid = multiplier + applied + local_n * multiplier - adjoint_forcing
            adjoint["resid"] = resid
            adjoint["delta"] = -RELAXATION * resid / diagonal_n
        else:
            delta = adjoint["delta"]
            image = delta + applied + local_n * delta
            adjoint["delta"] = delta + RELAXATION * (-adjoint["resid"] - image) / diagonal_n
        if closing:
            adjoint["mult"] = adjoint["mult"] + adjoint["delta"]

    forward_plan = []
    adjoint_plan = []
    for newton_step in range(OUTER):
        forward_plan.append(("res", INNER == 1))
        if newton_step > 0:
            adjoint_plan.append(("res", INNER == 1))
        for inner_step in range(INNER - 1):
            forward_plan.append(("lin", inner_step == INNER - 2))
            adjoint_plan.append(("lin", inner_step == INNER - 2))
    forward_plan.append(("final", False))
    for position in range(max(len(forward_plan), len(adjoint_plan))):
        pending_tasks = []
        pending_tasks.append(
            forward_task(
                forward["delta"] if forward_plan[position][0] == "lin" else forward["state"]
            )
        )
        if position < len(adjoint_plan):
            pending_tasks.append(
                adjoint_task(
                    adjoint["delta"] if adjoint_plan[position][0] == "lin" else adjoint["mult"]
                )
            )
        results = run_tasks(pending_tasks)
        offset = 0
        forward_update(forward_plan[position][0], forward_plan[position][1], results[0])
        offset = 1
        if position < len(adjoint_plan):
            adjoint_update(adjoint_plan[position][0], adjoint_plan[position][1], results[offset])
    final_state = forward["state"]
    final_resid = forward["final"]
    multiplier = adjoint["mult"]
    adjoint_state = multiplier + observation_weight * (final_state - observations)
    return (final_state, final_resid, adjoint_state)


def solution(mesh):
    in_specs = (
        P(None, "gy", "gx"),
        P(None, "gy", "gx"),
        P(None, "gy", "gx"),
        P(None, "gy", "gx"),
        P(None, "gy", "gx"),
        P(None, "gy", "gx"),
        P(None, "gy", "gx"),
        P(),
        P(),
        P(None, "gy", "gx"),
        P(None, "gy", "gx"),
        P(None, "gy", "gx"),
        P(),
    )
    out_specs = (P(None, "gy", "gx"), P(None, "gy", "gx"), P(None, "gy", "gx"))
    return jax.shard_map(
        per_device, mesh=mesh, in_specs=in_specs, out_specs=out_specs, check_vma=False
    )
```

profile of v0, /device:TPU:6, one launch (start us, length us, event | category | flops | bytes accessed | tf_op | source)
XLA Modules:
  0.0 238.8 jit_solution(16429688565361268825)
XLA Ops:
  0.7 0.9 broadcast_multiply_fusion
  1.7 1.9 collective-permute-start.1
  4.8 3.6 %collective-permute-start = (f32[2,16,8,1]{1,2,3,0:T(8,128)S(1)}, f32[2,16,8,1]{1,2,3,0:T(8,128)S(1)}, u32[]{:S(2)}, u32[]{:S(2)}) collective-permute-start(f32[2,16,8,1]{1,2,3,0:T(8,128)S(1)} %pad_maximum_fusion.33), channel_id=1, source_target_pairs={{0,32},{32,64},{64,96},{96,128},{128,160},{160,192},{192,224},{224... | collective-permute-start | bytes 3080 | tf_op jit(solution)/shard_map/ppermute | solution.py:33
  9.4 18.2 %collective-permute-done = f32[2,16,8,1]{1,2,3,0:T(8,128)S(1)} collective-permute-done((f32[2,16,8,1]{1,2,3,0:T(8,128)S(1)}, f32[2,16,8,1]{1,2,3,0:T(8,128)S(1)}, u32[]{:S(2)}, u32[]{:S(2)}) %collective-permute-start) | collective-permute-done | bytes 1056 | tf_op jit(solution)/shard_map/ppermute | solution.py:33
  30.0 1.9 collective-permute-start.2
  31.9 9.9 %collective-permute-start.3 = (f32[2,16,8,1]{3,2,1,0:T(8,128)S(1)}, f32[2,16,8,1]{3,2,1,0:T(8,128)S(1)}, u32[]{:S(2)}, u32[]{:S(2)}) collective-permute-start(f32[2,16,8,1]{3,2,1,0:T(8,128)S(1)} %get-tuple-element.150), channel_id=1, source_target_pairs={{32,0},{64,32},{96,64},{128,96},{160,128},{192,160},{224,192},{256... | collective-permute-start | bytes 3080 | tf_op jit(solution)/shard_map/ppermute | solution.py:26
  42.1 2.0 collective-permute-start.4
  44.2 6.2 %collective-permute-start.5 = (f32[2,16,1,128]{3,2,1,0:T(1,128)S(1)}, f32[2,16,1,128]{3,2,1,0:T(1,128)S(1)}, u32[]{:S(2)}, u32[]{:S(2)}) collective-permute-start(f32[2,16,1,128]{3,2,1,0:T(1,128)S(1)} %get-tuple-element.146), channel_id=1, source_target_pairs={{1,0},{2,1},{3,2},{4,3},{5,4},{6,5},{7,6},{8,7},{9,8},{10,9},{11,1... | collective-permute-start | bytes 49160 | tf_op jit(solution)/shard_map/ppermute | solution.py:26
  50.4 3.3 %collective-permute-done.3 = f32[2,16,8,1]{3,2,1,0:T(8,128)S(1)} collective-permute-done((f32[2,16,8,1]{3,2,1,0:T(8,128)S(1)}, f32[2,16,8,1]{3,2,1,0:T(8,128)S(1)}, u32[]{:S(2)}, u32[]{:S(2)}) %collective-permute-start.3) | collective-permute-done | bytes 1056 | tf_op jit(solution)/shard_map/ppermute | solution.py:26
  56.1 1.9 collective-permute-start.6
  58.1 10.2 %collective-permute-start.7 = (f32[2,16,8,1]{3,2,1,0:T(8,128)S(1)}, f32[2,16,8,1]{3,2,1,0:T(8,128)S(1)}, u32[]{:S(2)}, u32[]{:S(2)}) collective-permute-start(f32[2,16,8,1]{3,2,1,0:T(8,128)S(1)} %get-tuple-element.142), channel_id=1, source_target_pairs={{32,0},{64,32},{96,64},{128,96},{160,128},{192,160},{224,192},{256... | collective-permute-start | bytes 3080 | tf_op jit(solution)/shard_map/ppermute | solution.py:26
  68.4 1.9 collective-permute-start.8
  70.4 6.3 %collective-permute-start.9 = (f32[2,16,1,128]{3,2,1,0:T(1,128)S(1)}, f32[2,16,1,128]{3,2,1,0:T(1,128)S(1)}, u32[]{:S(2)}, u32[]{:S(2)}) collective-permute-start(f32[2,16,1,128]{3,2,1,0:T(1,128)S(1)} %get-tuple-element.138), channel_id=1, source_target_pairs={{1,0},{2,1},{3,2},{4,3},{5,4},{6,5},{7,6},{8,7},{9,8},{10,9},{11,1... | collective-permute-start | bytes 49160 | tf_op jit(solution)/shard_map/ppermute | solution.py:26
  77.2 1.8 collective-permute-done.8
  80.0 1.9 collective-permute-start.10
  81.9 9.9 %collective-permute-start.11 = (f32[2,16,8,1]{3,2,1,0:T(8,128)S(1)}, f32[2,16,8,1]{3,2,1,0:T(8,128)S(1)}, u32[]{:S(2)}, u32[]{:S(2)}) collective-permute-start(f32[2,16,8,1]{3,2,1,0:T(8,128)S(1)} %get-tuple-element.134), channel_id=1, source_target_pairs={{32,0},{64,32},{96,64},{128,96},{160,128},{192,160},{224,192},{256... | collective-permute-start | bytes 3080 | tf_op jit(solution)/shard_map/ppermute | solution.py:26
  92.0 1.9 collective-permute-start.12
  93.9 6.3 %collective-permute-start.13 = (f32[2,16,1,128]{3,2,1,0:T(1,128)S(1)}, f32[2,16,1,128]{3,2,1,0:T(1,128)S(1)}, u32[]{:S(2)}, u32[]{:S(2)}) collective-permute-start(f32[2,16,1,128]{3,2,1,0:T(1,128)S(1)} %get-tuple-element.130), channel_id=1, source_target_pairs={{1,0},{2,1},{3,2},{4,3},{5,4},{6,5},{7,6},{8,7},{9,8},{10,9},{11,1... | collective-permute-start | bytes 49160 | tf_op jit(solution)/shard_map/ppermute | solution.py:26
  102.7 1.9 collective-permute-start.14
  104.6 9.9 %collective-permute-start.15 = (f32[2,16,8,1]{3,2,1,0:T(8,128)S(1)}, f32[2,16,8,1]{3,2,1,0:T(8,128)S(1)}, u32[]{:S(2)}, u32[]{:S(2)}) collective-permute-start(f32[2,16,8,1]{3,2,1,0:T(8,128)S(1)} %get-tuple-element.122), channel_id=1, source_target_pairs={{32,0},{64,32},{96,64},{128,96},{160,128},{192,160},{224,192},{256... | collective-permute-start | bytes 3080 | tf_op jit(solution)/shard_map/ppermute | solution.py:26
  114.7 1.9 collective-permute-start.16
  116.6 6.3 %collective-permute-start.17 = (f32[2,16,1,128]{3,2,1,0:T(1,128)S(1)}, f32[2,16,1,128]{3,2,1,0:T(1,128)S(1)}, u32[]{:S(2)}, u32[]{:S(2)}) collective-permute-start(f32[2,16,1,128]{3,2,1,0:T(1,128)S(1)} %get-tuple-element.126), channel_id=1, source_target_pairs={{1,0},{2,1},{3,2},{4,3},{5,4},{6,5},{7,6},{8,7},{9,8},{10,9},{11,1... | collective-permute-start | bytes 49160 | tf_op jit(solution)/shard_map/ppermute | solution.py:26
  123.5 0.9 collective-permute-done.17
  125.4 1.9 collective-permute-start.18
  127.3 9.9 %collective-permute-start.19 = (f32[2,16,8,1]{3,2,1,0:T(8,128)S(1)}, f32[2,16,8,1]{3,2,1,0:T(8,128)S(1)}, u32[]{:S(2)}, u32[]{:S(2)}) collective-permute-start(f32[2,16,8,1]{3,2,1,0:T(8,128)S(1)} %get-tuple-element.118), channel_id=1, source_target_pairs={{32,0},{64,32},{96,64},{128,96},{160,128},{192,160},{224,192},{256... | collective-permute-start | bytes 3080 | tf_op jit(solution)/shard_map/ppermute | solution.py:26
  137.4 1.9 collective-permute-start.20
  139.3 6.3 %collective-permute-start.21 = (f32[2,16,1,128]{3,2,1,0:T(1,128)S(1)}, f32[2,16,1,128]{3,2,1,0:T(1,128)S(1)}, u32[]{:S(2)}, u32[]{:S(2)}) collective-permute-start(f32[2,16,1,128]{3,2,1,0:T(1,128)S(1)} %get-tuple-element.114), channel_id=1, source_target_pairs={{1,0},{2,1},{3,2},{4,3},{5,4},{6,5},{7,6},{8,7},{9,8},{10,9},{11,1... | collective-permute-start | bytes 49160 | tf_op jit(solution)/shard_map/ppermute | solution.py:26
  146.2 0.9 collective-permute-done.21
  148.1 1.9 collective-permute-start.22
  150.1 9.9 %collective-permute-start.23 = (f32[2,16,8,1]{3,2,1,0:T(8,128)S(1)}, f32[2,16,8,1]{3,2,1,0:T(8,128)S(1)}, u32[]{:S(2)}, u32[]{:S(2)}) collective-permute-start(f32[2,16,8,1]{3,2,1,0:T(8,128)S(1)} %get-tuple-element.110), channel_id=1, source_target_pairs={{32,0},{64,32},{96,64},{128,96},{160,128},{192,160},{224,192},{256... | collective-permute-start | bytes 3080 | tf_op jit(solution)/shard_map/ppermute | solution.py:26
  160.1 1.9 collective-permute-start.24
  162.1 6.3 %collective-permute-start.25 = (f32[2,16,1,128]{3,2,1,0:T(1,128)S(1)}, f32[2,16,1,128]{3,2,1,0:T(1,128)S(1)}, u32[]{:S(2)}, u32[]{:S(2)}) collective-permute-start(f32[2,16,1,128]{3,2,1,0:T(1,128)S(1)} %get-tuple-element.106), channel_id=1, source_target_pairs={{1,0},{2,1},{3,2},{4,3},{5,4},{6,5},{7,6},{8,7},{9,8},{10,9},{11,1... | collective-permute-start | bytes 49160 | tf_op jit(solution)/shard_map/ppermute | solution.py:26
  168.9 0.9 collective-permute-done.25
  170.8 1.9 collective-permute-start.26
  172.8 9.9 %collective-permute-start.27 = (f32[2,16,8,1]{3,2,1,0:T(8,128)S(1)}, f32[2,16,8,1]{3,2,1,0:T(8,128)S(1)}, u32[]{:S(2)}, u32[]{:S(2)}) collective-permute-start(f32[2,16,8,1]{3,2,1,0:T(8,128)S(1)} %get-tuple-element.102), channel_id=1, source_target_pairs={{32,0},{64,32},{96,64},{128,96},{160,128},{192,160},{224,192},{256... | collective-permute-start | bytes 3080 | tf_op jit(solution)/shard_map/ppermute | solution.py:26
  182.9 1.9 collective-permute-start.28
  184.8 6.3 %collective-permute-start.29 = (f32[2,16,1,128]{3,2,1,0:T(1,128)S(1)}, f32[2,16,1,128]{3,2,1,0:T(1,128)S(1)}, u32[]{:S(2)}, u32[]{:S(2)}) collective-permute-start(f32[2,16,1,128]{3,2,1,0:T(1,128)S(1)} %get-tuple-element.98), channel_id=1, source_target_pairs={{1,0},{2,1},{3,2},{4,3},{5,4},{6,5},{7,6},{8,7},{9,8},{10,9},{11,1... | collective-permute-start | bytes 49160 | tf_op jit(solution)/shard_map/ppermute | solution.py:26
  191.6 0.9 collective-permute-done.29
  193.0 1.9 collective-permute-start.30
  195.0 9.9 %collective-permute-start.31 = (f32[1,16,8,1]{3,2,1,0:T(8,128)S(1)}, f32[1,16,8,1]{3,2,1,0:T(8,128)S(1)}, u32[]{:S(2)}, u32[]{:S(2)}) collective-permute-start(f32[1,16,8,1]{3,2,1,0:T(8,128)S(1)} %get-tuple-element.156), channel_id=1, source_target_pairs={{32,0},{64,32},{96,64},{128,96},{160,128},{192,160},{224,192},{256... | collective-permute-start | bytes 1544 | tf_op jit(solution)/shard_map/ppermute | solution.py:26
  204.9 1.9 collective-permute-start.32
  206.8 6.3 %collective-permute-start.33 = (f32[1,16,1,128]{3,2,1,0:T(1,128)S(1)}, f32[1,16,1,128]{3,2,1,0:T(1,128)S(1)}, u32[]{:S(2)}, u32[]{:S(2)}) collective-permute-start(f32[1,16,1,128]{3,2,1,0:T(1,128)S(1)} %get-tuple-element.158), channel_id=1, source_target_pairs={{1,0},{2,1},{3,2},{4,3},{5,4},{6,5},{7,6},{8,7},{9,8},{10,9},{11,1... | collective-permute-start | bytes 24584 | tf_op jit(solution)/shard_map/ppermute | solution.py:26
  213.5 1.0 collective-permute-done.33
  216.4 1.9 collective-permute-start.34
  218.3 9.9 %collective-permute-start.35 = (f32[1,16,8,1]{3,2,1,0:T(8,128)S(1)}, f32[1,16,8,1]{3,2,1,0:T(8,128)S(1)}, u32[]{:S(2)}, u32[]{:S(2)}) collective-permute-start(f32[1,16,8,1]{3,2,1,0:T(8,128)S(1)} %get-tuple-element.152), channel_id=1, source_target_pairs={{32,0},{64,32},{96,64},{128,96},{160,128},{192,160},{224,192},{256... | collective-permute-start | bytes 1544 | tf_op jit(solution)/shard_map/ppermute | solution.py:26
  228.3 1.9 collective-permute-start.36
  230.3 6.3 %collective-permute-start.37 = (f32[1,16,1,128]{3,2,1,0:T(1,128)S(1)}, f32[1,16,1,128]{3,2,1,0:T(1,128)S(1)}, u32[]{:S(2)}, u32[]{:S(2)}) collective-permute-start(f32[1,16,1,128]{3,2,1,0:T(1,128)S(1)} %get-tuple-element.154), channel_id=1, source_target_pairs={{1,0},{2,1},{3,2},{4,3},{5,4},{6,5},{7,6},{8,7},{9,8},{10,9},{11,1... | collective-permute-start | bytes 24584 | tf_op jit(solution)/shard_map/ppermute | solution.py:26
  237.0 1.0 collective-permute-done.37
  (219 shorter events, 19.3 us)
Async XLA Ops:
  0.6 1.0 copy-start.10
  1.6 2.0 copy-start
  1.7 26.2 %collective-permute-start.1 = (f32[2,16,1,128]{3,1,2,0:T(8,128)S(1)}, f32[2,16,1,128]{3,1,2,0:T(8,128)S(1)}, u32[]{:S(2)}, u32[]{:S(2)}) collective-permute-start(f32[2,16,1,128]{3,1,2,0:T(8,128)S(1)} %pad_maximum_fusion.32), channel_id=1, source_target_pairs={{0,1},{1,2},{2,3},{3,4},{4,5},{5,6},{6,7},{7,8},{8,9},{9,10},{10,1... | collective-permute-start | bytes 49160 | tf_op jit(solution)/shard_map/ppermute | solution.py:39
  3.7 0.8 copy-start.1
  4.8 3.6 %copy-start.11 = (f32[16]{0:T(128)S(1)}, f32[16]{0:T(128)}, u32[]{:S(2)}) copy-start(f32[16]{0:T(128)} %param.20) | copy-start | bytes 196
  4.8 22.9 %collective-permute-start = (f32[2,16,8,1]{1,2,3,0:T(8,128)S(1)}, f32[2,16,8,1]{1,2,3,0:T(8,128)S(1)}, u32[]{:S(2)}, u32[]{:S(2)}) collective-permute-start(f32[2,16,8,1]{1,2,3,0:T(8,128)S(1)} %pad_maximum_fusion.33), channel_id=1, source_target_pairs={{0,32},{32,64},{64,96},{96,128},{128,160},{160,192},{192,224},{224... | collective-permute-start | bytes 3080 | tf_op jit(solution)/shard_map/ppermute | solution.py:33
  27.8 0.8 copy-start.3
  28.8 0.8 copy-start.2
  30.0 20.4 %collective-permute-start.2 = (f32[2,16,8,1]{3,2,1,0:T(8,128)S(1)}, f32[2,16,8,1]{3,2,1,0:T(8,128)S(1)}, u32[]{:S(2)}, u32[]{:S(2)}) collective-permute-start(f32[2,16,8,1]{3,2,1,0:T(8,128)S(1)} %get-tuple-element.149), channel_id=1, source_target_pairs={{0,32},{32,64},{64,96},{96,128},{128,160},{160,192},{192,224},{224... | collective-permute-start | bytes 3080 | tf_op jit(solution)/shard_map/ppermute | solution.py:23
  31.9 21.7 %collective-permute-start.3 = (f32[2,16,8,1]{3,2,1,0:T(8,128)S(1)}, f32[2,16,8,1]{3,2,1,0:T(8,128)S(1)}, u32[]{:S(2)}, u32[]{:S(2)}) collective-permute-start(f32[2,16,8,1]{3,2,1,0:T(8,128)S(1)} %get-tuple-element.150), channel_id=1, source_target_pairs={{32,0},{64,32},{96,64},{128,96},{160,128},{192,160},{224,192},{256... | collective-permute-start | bytes 3080 | tf_op jit(solution)/shard_map/ppermute | solution.py:26
  42.1 12.3 %collective-permute-start.4 = (f32[2,16,1,128]{3,2,1,0:T(1,128)S(1)}, f32[2,16,1,128]{3,2,1,0:T(1,128)S(1)}, u32[]{:S(2)}, u32[]{:S(2)}) collective-permute-start(f32[2,16,1,128]{3,2,1,0:T(1,128)S(1)} %get-tuple-element.145), channel_id=1, source_target_pairs={{0,1},{1,2},{2,3},{3,4},{4,5},{5,6},{6,7},{7,8},{8,9},{9,10},{10,1... | collective-permute-start | bytes 49160 | tf_op jit(solution)/shard_map/ppermute | solution.py:23
  44.2 10.2 %collective-permute-start.5 = (f32[2,16,1,128]{3,2,1,0:T(1,128)S(1)}, f32[2,16,1,128]{3,2,1,0:T(1,128)S(1)}, u32[]{:S(2)}, u32[]{:S(2)}) collective-permute-start(f32[2,16,1,128]{3,2,1,0:T(1,128)S(1)} %get-tuple-element.146), channel_id=1, source_target_pairs={{1,0},{2,1},{3,2},{4,3},{5,4},{6,5},{7,6},{8,7},{9,8},{10,9},{11,1... | collective-permute-start | bytes 49160 | tf_op jit(solution)/shard_map/ppermute | solution.py:26
  54.7 0.8 copy-start.6
  56.1 20.6 %collective-permute-start.6 = (f32[2,16,8,1]{3,2,1,0:T(8,128)S(1)}, f32[2,16,8,1]{3,2,1,0:T(8,128)S(1)}, u32[]{:S(2)}, u32[]{:S(2)}) collective-permute-start(f32[2,16,8,1]{3,2,1,0:T(8,128)S(1)} %get-tuple-element.141), channel_id=1, source_target_pairs={{0,32},{32,64},{64,96},{96,128},{128,160},{160,192},{192,224},{224... | collective-permute-start | bytes 3080 | tf_op jit(solution)/shard_map/ppermute | solution.py:23
  58.1 18.7 %collective-permute-start.7 = (f32[2,16,8,1]{3,2,1,0:T(8,128)S(1)}, f32[2,16,8,1]{3,2,1,0:T(8,128)S(1)}, u32[]{:S(2)}, u32[]{:S(2)}) collective-permute-start(f32[2,16,8,1]{3,2,1,0:T(8,128)S(1)} %get-tuple-element.142), channel_id=1, source_target_pairs={{32,0},{64,32},{96,64},{128,96},{160,128},{192,160},{224,192},{256... | collective-permute-start | bytes 3080 | tf_op jit(solution)/shard_map/ppermute | solution.py:26
  68.4 10.5 %collective-permute-start.8 = (f32[2,16,1,128]{3,2,1,0:T(1,128)S(1)}, f32[2,16,1,128]{3,2,1,0:T(1,128)S(1)}, u32[]{:S(2)}, u32[]{:S(2)}) collective-permute-start(f32[2,16,1,128]{3,2,1,0:T(1,128)S(1)} %get-tuple-element.137), channel_id=1, source_target_pairs={{0,1},{1,2},{2,3},{3,4},{4,5},{5,6},{6,7},{7,8},{8,9},{9,10},{10,1... | collective-permute-start | bytes 49160 | tf_op jit(solution)/shard_map/ppermute | solution.py:23
  70.4 8.6 %collective-permute-start.9 = (f32[2,16,1,128]{3,2,1,0:T(1,128)S(1)}, f32[2,16,1,128]{3,2,1,0:T(1,128)S(1)}, u32[]{:S(2)}, u32[]{:S(2)}) collective-permute-start(f32[2,16,1,128]{3,2,1,0:T(1,128)S(1)} %get-tuple-element.138), channel_id=1, source_target_pairs={{1,0},{2,1},{3,2},{4,3},{5,4},{6,5},{7,6},{8,7},{9,8},{10,9},{11,1... | collective-permute-start | bytes 49160 | tf_op jit(solution)/shard_map/ppermute | solution.py:26
  80.0 20.3 %collective-permute-start.10 = (f32[2,16,8,1]{3,2,1,0:T(8,128)S(1)}, f32[2,16,8,1]{3,2,1,0:T(8,128)S(1)}, u32[]{:S(2)}, u32[]{:S(2)}) collective-permute-start(f32[2,16,8,1]{3,2,1,0:T(8,128)S(1)} %get-tuple-element.133), channel_id=1, source_target_pairs={{0,32},{32,64},{64,96},{96,128},{128,160},{160,192},{192,224},{224... | collective-permute-start | bytes 3080 | tf_op jit(solution)/shard_map/ppermute | solution.py:23
  81.9 18.4 %collective-permute-start.11 = (f32[2,16,8,1]{3,2,1,0:T(8,128)S(1)}, f32[2,16,8,1]{3,2,1,0:T(8,128)S(1)}, u32[]{:S(2)}, u32[]{:S(2)}) collective-permute-start(f32[2,16,8,1]{3,2,1,0:T(8,128)S(1)} %get-tuple-element.134), channel_id=1, source_target_pairs={{32,0},{64,32},{96,64},{128,96},{160,128},{192,160},{224,192},{256... | collective-permute-start | bytes 3080 | tf_op jit(solution)/shard_map/ppermute | solution.py:26
  92.0 9.6 %collective-permute-start.12 = (f32[2,16,1,128]{3,2,1,0:T(1,128)S(1)}, f32[2,16,1,128]{3,2,1,0:T(1,128)S(1)}, u32[]{:S(2)}, u32[]{:S(2)}) collective-permute-start(f32[2,16,1,128]{3,2,1,0:T(1,128)S(1)} %get-tuple-element.129), channel_id=1, source_target_pairs={{0,1},{1,2},{2,3},{3,4},{4,5},{5,6},{6,7},{7,8},{8,9},{9,10},{10,1... | collective-permute-start | bytes 49160 | tf_op jit(solution)/shard_map/ppermute | solution.py:23
  93.9 7.8 %collective-permute-start.13 = (f32[2,16,1,128]{3,2,1,0:T(1,128)S(1)}, f32[2,16,1,128]{3,2,1,0:T(1,128)S(1)}, u32[]{:S(2)}, u32[]{:S(2)}) collective-permute-start(f32[2,16,1,128]{3,2,1,0:T(1,128)S(1)} %get-tuple-element.130), channel_id=1, source_target_pairs={{1,0},{2,1},{3,2},{4,3},{5,4},{6,5},{7,6},{8,7},{9,8},{10,9},{11,1... | collective-permute-start | bytes 49160 | tf_op jit(solution)/shard_map/ppermute | solution.py:26
  102.7 20.3 %collective-permute-start.14 = (f32[2,16,8,1]{3,2,1,0:T(8,128)S(1)}, f32[2,16,8,1]{3,2,1,0:T(8,128)S(1)}, u32[]{:S(2)}, u32[]{:S(2)}) collective-permute-start(f32[2,16,8,1]{3,2,1,0:T(8,128)S(1)} %get-tuple-element.121), channel_id=1, source_target_pairs={{0,32},{32,64},{64,96},{96,128},{128,160},{160,192},{192,224},{224... | collective-permute-start | bytes 3080 | tf_op jit(solution)/shard_map/ppermute | solution.py:23
  104.6 18.4 %collective-permute-start.15 = (f32[2,16,8,1]{3,2,1,0:T(8,128)S(1)}, f32[2,16,8,1]{3,2,1,0:T(8,128)S(1)}, u32[]{:S(2)}, u32[]{:S(2)}) collective-permute-start(f32[2,16,8,1]{3,2,1,0:T(8,128)S(1)} %get-tuple-element.122), channel_id=1, source_target_pairs={{32,0},{64,32},{96,64},{128,96},{160,128},{192,160},{224,192},{256... | collective-permute-start | bytes 3080 | tf_op jit(solution)/shard_map/ppermute | solution.py:26
  114.7 8.8 %collective-permute-start.16 = (f32[2,16,1,128]{3,2,1,0:T(1,128)S(1)}, f32[2,16,1,128]{3,2,1,0:T(1,128)S(1)}, u32[]{:S(2)}, u32[]{:S(2)}) collective-permute-start(f32[2,16,1,128]{3,2,1,0:T(1,128)S(1)} %get-tuple-element.125), channel_id=1, source_target_pairs={{0,1},{1,2},{2,3},{3,4},{4,5},{5,6},{6,7},{7,8},{8,9},{9,10},{10,1... | collective-permute-start | bytes 49160 | tf_op jit(solution)/shard_map/ppermute | solution.py:23
  116.6 7.8 %collective-permute-start.17 = (f32[2,16,1,128]{3,2,1,0:T(1,128)S(1)}, f32[2,16,1,128]{3,2,1,0:T(1,128)S(1)}, u32[]{:S(2)}, u32[]{:S(2)}) collective-permute-start(f32[2,16,1,128]{3,2,1,0:T(1,128)S(1)} %get-tuple-element.126), channel_id=1, source_target_pairs={{1,0},{2,1},{3,2},{4,3},{5,4},{6,5},{7,6},{8,7},{9,8},{10,9},{11,1... | collective-permute-start | bytes 49160 | tf_op jit(solution)/shard_map/ppermute | solution.py:26
  125.4 20.3 %collective-permute-start.18 = (f32[2,16,8,1]{3,2,1,0:T(8,128)S(1)}, f32[2,16,8,1]{3,2,1,0:T(8,128)S(1)}, u32[]{:S(2)}, u32[]{:S(2)}) collective-permute-start(f32[2,16,8,1]{3,2,1,0:T(8,128)S(1)} %get-tuple-element.117), channel_id=1, source_target_pairs={{0,32},{32,64},{64,96},{96,128},{128,160},{160,192},{192,224},{224... | collective-permute-start | bytes 3080 | tf_op jit(solution)/shard_map/ppermute | solution.py:23
  127.3 18.4 %collective-permute-start.19 = (f32[2,16,8,1]{3,2,1,0:T(8,128)S(1)}, f32[2,16,8,1]{3,2,1,0:T(8,128)S(1)}, u32[]{:S(2)}, u32[]{:S(2)}) collective-permute-start(f32[2,16,8,1]{3,2,1,0:T(8,128)S(1)} %get-tuple-element.118), channel_id=1, source_target_pairs={{32,0},{64,32},{96,64},{128,96},{160,128},{192,160},{224,192},{256... | collective-permute-start | bytes 3080 | tf_op jit(solution)/shard_map/ppermute | solution.py:26
  137.4 8.8 %collective-permute-start.20 = (f32[2,16,1,128]{3,2,1,0:T(1,128)S(1)}, f32[2,16,1,128]{3,2,1,0:T(1,128)S(1)}, u32[]{:S(2)}, u32[]{:S(2)}) collective-permute-start(f32[2,16,1,128]{3,2,1,0:T(1,128)S(1)} %get-tuple-element.113), channel_id=1, source_target_pairs={{0,1},{1,2},{2,3},{3,4},{4,5},{5,6},{6,7},{7,8},{8,9},{9,10},{10,1... | collective-permute-start | bytes 49160 | tf_op jit(solution)/shard_map/ppermute | solution.py:23
  139.3 7.8 %collective-permute-start.21 = (f32[2,16,1,128]{3,2,1,0:T(1,128)S(1)}, f32[2,16,1,128]{3,2,1,0:T(1,128)S(1)}, u32[]{:S(2)}, u32[]{:S(2)}) collective-permute-start(f32[2,16,1,128]{3,2,1,0:T(1,128)S(1)} %get-tuple-element.114), channel_id=1, source_target_pairs={{1,0},{2,1},{3,2},{4,3},{5,4},{6,5},{7,6},{8,7},{9,8},{10,9},{11,1... | collective-permute-start | bytes 49160 | tf_op jit(solution)/shard_map/ppermute | solution.py:26
  148.1 20.3 %collective-permute-start.22 = (f32[2,16,8,1]{3,2,1,0:T(8,128)S(1)}, f32[2,16,8,1]{3,2,1,0:T(8,128)S(1)}, u32[]{:S(2)}, u32[]{:S(2)}) collective-permute-start(f32[2,16,8,1]{3,2,1,0:T(8,128)S(1)} %get-tuple-element.109), channel_id=1, source_target_pairs={{0,32},{32,64},{64,96},{96,128},{128,160},{160,192},{192,224},{224... | collective-permute-start | bytes 3080 | tf_op jit(solution)/shard_map/ppermute | solution.py:23
  150.1 18.4 %collective-permute-start.23 = (f32[2,16,8,1]{3,2,1,0:T(8,128)S(1)}, f32[2,16,8,1]{3,2,1,0:T(8,128)S(1)}, u32[]{:S(2)}, u32[]{:S(2)}) collective-permute-start(f32[2,16,8,1]{3,2,1,0:T(8,128)S(1)} %get-tuple-element.110), channel_id=1, source_target_pairs={{32,0},{64,32},{96,64},{128,96},{160,128},{192,160},{224,192},{256... | collective-permute-start | bytes 3080 | tf_op jit(solution)/shard_map/ppermute | solution.py:26
  160.1 8.8 %collective-permute-start.24 = (f32[2,16,1,128]{3,2,1,0:T(1,128)S(1)}, f32[2,16,1,128]{3,2,1,0:T(1,128)S(1)}, u32[]{:S(2)}, u32[]{:S(2)}) collective-permute-start(f32[2,16,1,128]{3,2,1,0:T(1,128)S(1)} %get-tuple-element.105), channel_id=1, source_target_pairs={{0,1},{1,2},{2,3},{3,4},{4,5},{5,6},{6,7},{7,8},{8,9},{9,10},{10,1... | collective-permute-start | bytes 49160 | tf_op jit(solution)/shard_map/ppermute | solution.py:23
  162.1 7.8 %collective-permute-start.25 = (f32[2,16,1,128]{3,2,1,0:T(1,128)S(1)}, f32[2,16,1,128]{3,2,1,0:T(1,128)S(1)}, u32[]{:S(2)}, u32[]{:S(2)}) collective-permute-start(f32[2,16,1,128]{3,2,1,0:T(1,128)S(1)} %get-tuple-element.106), channel_id=1, source_target_pairs={{1,0},{2,1},{3,2},{4,3},{5,4},{6,5},{7,6},{8,7},{9,8},{10,9},{11,1... | collective-permute-start | bytes 49160 | tf_op jit(solution)/shard_map/ppermute | solution.py:26
  170.8 20.3 %collective-permute-start.26 = (f32[2,16,8,1]{3,2,1,0:T(8,128)S(1)}, f32[2,16,8,1]{3,2,1,0:T(8,128)S(1)}, u32[]{:S(2)}, u32[]{:S(2)}) collective-permute-start(f32[2,16,8,1]{3,2,1,0:T(8,128)S(1)} %get-tuple-element.101), channel_id=1, source_target_pairs={{0,32},{32,64},{64,96},{96,128},{128,160},{160,192},{192,224},{224... | collective-permute-start | bytes 3080 | tf_op jit(solution)/shard_map/ppermute | solution.py:23
  172.8 18.4 %collective-permute-start.27 = (f32[2,16,8,1]{3,2,1,0:T(8,128)S(1)}, f32[2,16,8,1]{3,2,1,0:T(8,128)S(1)}, u32[]{:S(2)}, u32[]{:S(2)}) collective-permute-start(f32[2,16,8,1]{3,2,1,0:T(8,128)S(1)} %get-tuple-element.102), channel_id=1, source_target_pairs={{32,0},{64,32},{96,64},{128,96},{160,128},{192,160},{224,192},{256... | collective-permute-start | bytes 3080 | tf_op jit(solution)/shard_map/ppermute | solution.py:26
  182.9 8.8 %collective-permute-start.28 = (f32[2,16,1,128]{3,2,1,0:T(1,128)S(1)}, f32[2,16,1,128]{3,2,1,0:T(1,128)S(1)}, u32[]{:S(2)}, u32[]{:S(2)}) collective-permute-start(f32[2,16,1,128]{3,2,1,0:T(1,128)S(1)} %get-tuple-element.97), channel_id=1, source_target_pairs={{0,1},{1,2},{2,3},{3,4},{4,5},{5,6},{6,7},{7,8},{8,9},{9,10},{10,1... | collective-permute-start | bytes 49160 | tf_op jit(solution)/shard_map/ppermute | solution.py:23
  184.8 7.8 %collective-permute-start.29 = (f32[2,16,1,128]{3,2,1,0:T(1,128)S(1)}, f32[2,16,1,128]{3,2,1,0:T(1,128)S(1)}, u32[]{:S(2)}, u32[]{:S(2)}) collective-permute-start(f32[2,16,1,128]{3,2,1,0:T(1,128)S(1)} %get-tuple-element.98), channel_id=1, source_target_pairs={{1,0},{2,1},{3,2},{4,3},{5,4},{6,5},{7,6},{8,7},{9,8},{10,9},{11,1... | collective-permute-start | bytes 49160 | tf_op jit(solution)/shard_map/ppermute | solution.py:26
  193.0 20.2 %collective-permute-start.30 = (f32[1,16,8,1]{3,2,1,0:T(8,128)S(1)}, f32[1,16,8,1]{3,2,1,0:T(8,128)S(1)}, u32[]{:S(2)}, u32[]{:S(2)}) collective-permute-start(f32[1,16,8,1]{3,2,1,0:T(8,128)S(1)} %get-tuple-element.155), channel_id=1, source_target_pairs={{0,32},{32,64},{64,96},{96,128},{128,160},{160,192},{192,224},{224... | collective-permute-start | bytes 1544 | tf_op jit(solution)/shard_map/ppermute | solution.py:23
  195.0 18.3 %collective-permute-start.31 = (f32[1,16,8,1]{3,2,1,0:T(8,128)S(1)}, f32[1,16,8,1]{3,2,1,0:T(8,128)S(1)}, u32[]{:S(2)}, u32[]{:S(2)}) collective-permute-start(f32[1,16,8,1]{3,2,1,0:T(8,128)S(1)} %get-tuple-element.156), channel_id=1, source_target_pairs={{32,0},{64,32},{96,64},{128,96},{160,128},{192,160},{224,192},{256... | collective-permute-start | bytes 1544 | tf_op jit(solution)/shard_map/ppermute | solution.py:26
  204.9 8.6 %collective-permute-start.32 = (f32[1,16,1,128]{3,2,1,0:T(1,128)S(1)}, f32[1,16,1,128]{3,2,1,0:T(1,128)S(1)}, u32[]{:S(2)}, u32[]{:S(2)}) collective-permute-start(f32[1,16,1,128]{3,2,1,0:T(1,128)S(1)} %get-tuple-element.157), channel_id=1, source_target_pairs={{0,1},{1,2},{2,3},{3,4},{4,5},{5,6},{6,7},{7,8},{8,9},{9,10},{10,1... | collective-permute-start | bytes 24584 | tf_op jit(solution)/shard_map/ppermute | solution.py:23
  206.8 7.7 %collective-permute-start.33 = (f32[1,16,1,128]{3,2,1,0:T(1,128)S(1)}, f32[1,16,1,128]{3,2,1,0:T(1,128)S(1)}, u32[]{:S(2)}, u32[]{:S(2)}) collective-permute-start(f32[1,16,1,128]{3,2,1,0:T(1,128)S(1)} %get-tuple-element.158), channel_id=1, source_target_pairs={{1,0},{2,1},{3,2},{4,3},{5,4},{6,5},{7,6},{8,7},{9,8},{10,9},{11,1... | collective-permute-start | bytes 24584 | tf_op jit(solution)/shard_map/ppermute | solution.py:26
  214.6 0.8 copy-start.8
  214.6 0.9 copy-start.9
  216.3 21.8 %copy-start.4 = (f32[16,8,128]{2,1,0:T(8,128)}, f32[16,8,128]{2,1,0:T(8,128)S(1)}, u32[]{:S(2)}) copy-start(f32[16,8,128]{2,1,0:T(8,128)S(1)} %get-tuple-element.4) | copy-start | bytes 196612
  216.4 20.2 %collective-permute-start.34 = (f32[1,16,8,1]{3,2,1,0:T(8,128)S(1)}, f32[1,16,8,1]{3,2,1,0:T(8,128)S(1)}, u32[]{:S(2)}, u32[]{:S(2)}) collective-permute-start(f32[1,16,8,1]{3,2,1,0:T(8,128)S(1)} %get-tuple-element.151), channel_id=1, source_target_pairs={{0,32},{32,64},{64,96},{96,128},{128,160},{160,192},{192,224},{224... | collective-permute-start | bytes 1544 | tf_op jit(solution)/shard_map/ppermute | solution.py:23
  218.3 18.3 %collective-permute-start.35 = (f32[1,16,8,1]{3,2,1,0:T(8,128)S(1)}, f32[1,16,8,1]{3,2,1,0:T(8,128)S(1)}, u32[]{:S(2)}, u32[]{:S(2)}) collective-permute-start(f32[1,16,8,1]{3,2,1,0:T(8,128)S(1)} %get-tuple-element.152), channel_id=1, source_target_pairs={{32,0},{64,32},{96,64},{128,96},{160,128},{192,160},{224,192},{256... | collective-permute-start | bytes 1544 | tf_op jit(solution)/shard_map/ppermute | solution.py:26
  228.3 8.6 %collective-permute-start.36 = (f32[1,16,1,128]{3,2,1,0:T(1,128)S(1)}, f32[1,16,1,128]{3,2,1,0:T(1,128)S(1)}, u32[]{:S(2)}, u32[]{:S(2)}) collective-permute-start(f32[1,16,1,128]{3,2,1,0:T(1,128)S(1)} %get-tuple-element.153), channel_id=1, source_target_pairs={{0,1},{1,2},{2,3},{3,4},{4,5},{5,6},{6,7},{7,8},{8,9},{9,10},{10,1... | collective-permute-start | bytes 24584 | tf_op jit(solution)/shard_map/ppermute | solution.py:23
  230.3 7.7 %collective-permute-start.37 = (f32[1,16,1,128]{3,2,1,0:T(1,128)S(1)}, f32[1,16,1,128]{3,2,1,0:T(1,128)S(1)}, u32[]{:S(2)}, u32[]{:S(2)}) collective-permute-start(f32[1,16,1,128]{3,2,1,0:T(1,128)S(1)} %get-tuple-element.154), channel_id=1, source_target_pairs={{1,0},{2,1},{3,2},{4,3},{5,4},{6,5},{7,6},{8,7},{9,8},{10,9},{11,1... | collective-permute-start | bytes 24584 | tf_op jit(solution)/shard_map/ppermute | solution.py:26
  (2 other events, 1.5 us)
where the time goes:
time: 241 us; the launch traced here: 239 us
  starting transfers between devices  187 us (78%)
  waiting for transfers between devices  30.3 us (13%)
  other arithmetic  13.4 us (6%)
  local copies, waits for them, and re-layouts  5.56 us (2%)
  between operations  2.72 us (1%)
    ppermute x18, starting transfers between devices, extended(): lax.ppermute(lax.slice_in_dim(block, 0, width, axis=dim), axis, backward)  147 us
    ppermute x18, starting transfers between devices, extended(): lax.ppermute(lax.slice_in_dim(block, block.shape[dim] - width, None, axis...  34.7 us
    ppermute x1, waiting for transfers between devices, shifted(): lax.ppermute(array, axis, [(i, (i + by) % size) for i in range(size)])  18.2 us
    ppermute x18, waiting for transfers between devices, extended(): lax.ppermute(lax.slice_in_dim(block, 0, width, axis=dim), axis, backward)  9.02 us
  transfers between devices with their start and end apart: 38, of which 12 were waited for; matrix products, arithmetic and copies ran while one was open for 2% of the time, Pallas kernels for 0%

commit v1 on v0

v1 whole, which is shorter than its diff:
```python
import functools
import math

import jax
import jax.numpy as jnp
from jax import lax
from jax.experimental import pallas as pl
from jax.experimental.pallas import tpu as pltpu
from jax.sharding import PartitionSpec as P

DAY_STEPS = 96
RELAXATION = 0.7
SLOT = 16
FIELDS = 8
C, S, ED, EW, ND, NW, TR, AF = range(8)


def lane_ids():
    return lax.broadcasted_iota(jnp.int32, (8, 128), 1)


def pack_kernel(last_ref, *refs):
    fields = refs[:FIELDS]
    bulk, to_east, to_west, far_north, far_south = refs[FIELDS:]
    levels = fields[0].shape[0]
    lanes = lane_ids()
    row = lax.broadcasted_iota(jnp.int32, (8, 128), 0)
    closed = jnp.where((row == 7) & (last_ref[0] == 1), 0.0, 1.0)
    for level in range(levels):
        east = jnp.zeros((8, 128), jnp.float32)
        west = jnp.zeros((8, 128), jnp.float32)
        for k in range(FIELDS):
            value = fields[k][level]
            if k in (ND, NW):
                value = value * closed
            bulk[k, level] = value
            slot = (lanes >= k * SLOT) & (lanes < (k + 1) * SLOT)
            east = jnp.where(slot, pltpu.roll(value, (k * SLOT + SLOT) % 128, 1), east)
            west = jnp.where(slot, pltpu.roll(value, k * SLOT, 1) if k else value, west)
            if k == C:
                far_south[level : level + 1] = value[0:1]
            if k in (C, ND, NW):
                place = {C: 0, ND: 1, NW: 2}[k] * levels + level
                far_north[place : place + 1] = value[7:8]
        to_east[level] = east
        to_west[level] = west


def solve_kernel(
    level_ref,
    damp_ref,
    cos_ref,
    own,
    south,
    north,
    from_west,
    from_east,
    corner_south,
    corner_north,
    far_south,
    far_north,
    observations,
    weight,
    out_state,
    out_resid,
    out_adjoint,
    check,
    force,
    a_c,
    diag,
    up_e,
    low_w,
    up_n,
    low_s,
    low_e,
    up_w,
    low_n,
    up_s,
    wt,
    ctr,
    g,
    d,
    x,
    aq_a,
    wt_a,
    ctr_a,
    g_a,
    d_a,
    mu,
):
    levels = check.shape[0]
    lanes = lane_ids()
    rows = lax.broadcasted_iota(jnp.int32, (24, 256), 0)

    def unroll_roll(value, shift):
        return value if shift % 128 == 0 else pltpu.roll(value, shift % 128, 1)

    def halo(k, west, east):
        left = unroll_roll(west, 128 - SLOT - k * SLOT)
        right = unroll_roll(east, -k * SLOT)
        return jnp.where(lanes < SLOT, right, jnp.where(lanes >= 128 - SLOT, left, 0.0))

    def gather(k, level):
        tiles = []
        for block, west, east in (
            (south, corner_south.at[0], corner_south.at[1]),
            (own, from_west, from_east),
            (north, corner_north.at[0], corner_north.at[1]),
        ):
            tiles.append(
                jnp.concatenate([block[k, level], halo(k, west[level], east[level])], axis=1)
            )
        return jnp.concatenate(tiles, axis=0)

    def wide(ref, index):
        line = ref[index : index + 1]
        line = jnp.concatenate([line, jnp.zeros_like(line)], axis=1)
        return jnp.broadcast_to(line, (24, 256))

    def to_e(v):
        return pltpu.roll(v, 255, 1)

    def to_w(v):
        return pltpu.roll(v, 1, 1)

    def to_n(v):
        return pltpu.roll(v, 23, 0)

    def to_s(v):
        return pltpu.roll(v, 1, 0)

    def up(level):
        return level_ref[level] if level < levels - 1 else None

    def down(level):
        return level_ref[level - 1] if level > 0 else None

    def pair(level):
        parts = [u for u in (up(level), down(level)) if u is not None]
        return sum(parts[1:], parts[0])

    def with_levels(total, level, below, above):
        if above is not None:
            total = total - up(level) * above
        if below is not None:
            total = total - down(level) * below
        return total

    def forward_sum(level, v, below, above, v_n=None, v_s=None):
        v_n = to_n(v) if v_n is None else v_n
        v_s = to_s(v) if v_s is None else v_s
        total = up_e[level] * to_e(v) - low_w[level] * to_w(v)
        total = total + (up_n[level] * v_n - low_s[level] * v_s)
        return with_levels(total, level, below, above)

    def adjoint_sum(level, v, below, above):
        total = up_w[level] * to_w(v) - low_e[level] * to_e(v)
        total = total + (up_s[level] * to_s(v) - low_n[level] * to_n(v))
        return with_levels(total, level, below, above)

    def sweep(field, body):
        below, here = None, field[0]
        for level in range(levels):
            above = field[level + 1] if level + 1 < levels else None
            body(level, here, below, above)
            below, here = here, above

    for level in range(levels):
        ed = gather(ED, level)
        ew = gather(EW, level) * 0.5
        nd = gather(ND, level)
        nw = gather(NW, level) * 0.5
        far_nd = wide(far_south, levels + level)
        far_nw = wide(far_south, 2 * levels + level) * 0.5
        first = rows == 0
        e_low, e_up, n_low, n_up = ew + ed, ew - ed, nw + nd, nw - nd
        w_low, w_up = to_w(e_low), to_w(e_up)
        s_low = jnp.where(first, far_nw + far_nd, to_s(n_low))
        s_up = jnp.where(first, far_nw - far_nd, to_s(n_up))
        up_e[level] = e_up
        low_e[level] = e_low
        up_w[level] = w_up
        low_w[level] = w_low
        up_n[level] = n_up
        low_n[level] = n_low
        up_s[level] = s_up
        low_s[level] = s_low
        center = (e_low - w_up) + (n_low - s_up) + pair(level)
        a_c[level] = center
        base = ed + to_w(ed) + nd + jnp.where(first, far_nd, to_s(nd)) + (1.0 + pair(level))
        diag[level] = base
        check[level] = gather(C, level)
        force[level] = gather(S, level) * cos_ref[...]
        tangent = jnp.tanh(gather(TR, level))
        local = damp_ref[level] * (1.0 - tangent * tangent)
        weight_a = RELAXATION / (base + local)
        af = gather(AF, level)
        diagonal = 1.0 + center + local
        aq_a[level] = diagonal
        wt_a[level] = weight_a
        ctr_a[level] = 1.0 - weight_a * diagonal
        start = weight_a * af
        g_a[level] = start
        d_a[level] = start

    def newton(level, v, resid, tangent):
        local = damp_ref[level] * (1.0 - tangent * tangent)
        w = RELAXATION / (diag[level] + local)
        wt[level] = w
        ctr[level] = 1.0 - w * (1.0 + a_c[level] + local)
        start = -(w * resid)
        g[level] = start
        d[level] = start

    def first_resid(level, v, below, above):
        tangent = jnp.tanh(v)
        v_s = jnp.where(rows == 0, wide(far_south, level), to_s(v))
        v_n = jnp.where(rows == 23, wide(far_north, level), to_n(v))
        total = forward_sum(level, v, below, above, v_n, v_s)
        resid = total + a_c[level] * v + damp_ref[level] * tangent - force[level]
        newton(level, v, resid, tangent)

    def forward_lin(level, v, below, above):
        total = forward_sum(level, v, below, above)
        d[level] = g[level] + ctr[level] * v - wt[level] * total

    def adjoint_lin(level, v, below, above):
        total = adjoint_sum(level, v, below, above)
        d_a[level] = g_a[level] + ctr_a[level] * v - wt_a[level] * total

    def relax(field, body):
        def step(_, carry):
            sweep(field, body)
            return carry

        lax.fori_loop(0, 3, step, 0)

    sweep(check, first_resid)
    relax(d, forward_lin)

    relax(d_a, adjoint_lin)
    for level in range(levels):
        x[level] = check[level] + d[level]
        mu[level] = d_a[level]

    def second_resid(level, v, below, above):
        tangent = jnp.tanh(v)
        total = forward_sum(level, v, below, above)
        moved = v - check[level]
        resid = moved + total + a_c[level] * v + damp_ref[level] * tangent - force[level]
        newton(level, v, resid, tangent)

    def adjoint_resid(level, v, below, above):
        total = adjoint_sum(level, v, below, above)
        af = g_a[level]
        start = af - wt_a[level] * (total + aq_a[level] * v)
        g_a[level] = start
        d_a[level] = start

    sweep(x, second_resid)
    relax(d, forward_lin)
    sweep(mu, adjoint_resid)
    relax(d_a, adjoint_lin)
    for level in range(levels):
        final = x[level] + d[level]
        x[level] = final
        state = final[8:16, :128]
        out_state[level] = state
        multiplier = mu[level, 8:16, :128] + d_a[level, 8:16, :128]
        out_adjoint[level] = multiplier + weight[level] * (state - observations[level])

    def final_resid(level, v, below, above):
        total = forward_sum(level, v, below, above)
        moved = v - check[level]
        resid = moved + total + a_c[level] * v + damp_ref[level] * jnp.tanh(v) - force[level]
        out_resid[level] = resid[8:16, :128]

    sweep(x, final_resid)


def vmem(count):
    return [pl.BlockSpec(memory_space=pltpu.VMEM) for _ in range(count)]


def shifted(array, axis, by, periodic):
    size = lax.axis_size(axis)
    pairs = [(i, (i + by) % size) for i in range(size) if periodic or 0 <= i + by < size]
    return lax.ppermute(array, axis, pairs)


def per_device(
    checkpoint,
    trajectory,
    adjoint_forcing,
    east_diffusion,
    north_diffusion,
    east_wind,
    north_wind,
    level_diffusion,
    damping,
    source,
    observations,
    observation_weight,
    step_index,
):
    levels, lat_rows, lon_cols = checkpoint.shape
    size_x = lax.axis_size("gx")
    size_y = lax.axis_size("gy")
    lane = jnp.arange(256, dtype=jnp.int32)
    column = lax.axis_index("gx") * lon_cols + lane - jnp.where(lane >= 192, 256, 0)
    column = jnp.remainder(column, lon_cols * size_x).astype(jnp.float32)
    phase = (
        2.0 * math.pi * column / (lon_cols * size_x)
        - 2.0 * math.pi * step_index[0].astype(jnp.float32) / DAY_STEPS
    )
    wave = jnp.cos(phase)[None, :]
    last = (lax.axis_index("gy") == size_y - 1).astype(jnp.int32)[None]
    tile = (levels, lat_rows, lon_cols)
    f32 = jnp.float32
    smem = pl.BlockSpec(memory_space=pltpu.SMEM)
    bulk, to_east, to_west, far_up, far_down = pl.pallas_call(
        pack_kernel,
        in_specs=[smem] + vmem(8),
        out_specs=vmem(5),
        out_shape=[
            jax.ShapeDtypeStruct((FIELDS,) + tile, f32),
            jax.ShapeDtypeStruct(tile, f32),
            jax.ShapeDtypeStruct(tile, f32),
            jax.ShapeDtypeStruct((3 * levels, lon_cols), f32),
            jax.ShapeDtypeStruct((levels, lon_cols), f32),
        ],
    )(
        last,
        checkpoint,
        source,
        east_diffusion,
        east_wind,
        north_diffusion,
        north_wind,
        trajectory,
        adjoint_forcing,
    )
    from_west = shifted(to_east, "gx", 1, True)
    from_east = shifted(to_west, "gx", -1, True)
    south = shifted(bulk, "gy", 1, False)
    north = shifted(bulk, "gy", -1, False)
    far_south = shifted(far_up, "gy", 2, False)
    far_north = shifted(far_down, "gy", -2, False)
    corners = jnp.stack([from_west, from_east])
    corner_south = shifted(corners, "gy", 1, False)
    corner_north = shifted(corners, "gy", -1, False)
    scratch = [pltpu.VMEM((levels, 24, 256), f32) for _ in range(23)]
    return tuple(
        pl.pallas_call(
            solve_kernel,
            in_specs=[smem, smem] + vmem(12),
            out_specs=vmem(3),
            out_shape=[jax.ShapeDtypeStruct(tile, f32)] * 3,
            scratch_shapes=scratch,
            compiler_params=pltpu.CompilerParams(vmem_limit_bytes=40 * 1024 * 1024),
        )(
            level_diffusion,
            damping,
            wave,
            bulk,
            south,
            north,
            from_west,
            from_east,
            corner_south,
            corner_north,
            far_south,
            far_north,
            observations,
            observation_weight,
        )
    )


def solution(mesh):
    spread = P(None, "gy", "gx")
    in_specs = (spread,) * 7 + (P(), P()) + (spread,) * 3 + (P(),)
    return jax.shard_map(
        per_device, mesh=mesh, in_specs=in_specs, out_specs=(spread,) * 3, check_vma=False
    )
```

time: 241 us -> 74.5 us (0.31)
  starting transfers between devices: 187 us -> 42.5 us
  other arithmetic: 13.4 us -> 0.07 us
  waiting for transfers between devices: 30.3 us -> 18.6 us
  Pallas kernels: 0 us -> 10.3 us
  local copies, waits for them, and re-layouts: 5.56 us -> 1.06 us
    ppermute x38 -> x8, starting transfers between devices: 187 us -> 42.5 us  [shifted(): return lax.ppermute(array, axis, pairs)]
    ppermute x38 -> x8, waiting for transfers between devices: 30.3 us -> 18.6 us  [shifted(): return lax.ppermute(array, axis, pairs)]
    pallas_call x0 -> x2, Pallas kernels: none -> 10.3 us  [the longest x1 8.26 us: per_device(): pl.pallas_call(solve_kernel, in_specs=[smem, smem] + vmem(12), out_specs=...]
    mul x26 -> x0, other arithmetic: 3.49 us -> none  [the longest x1 0.95 us: per_device(): north_masked = north_diffusion * row_mask]
    add x19 -> x0, other arithmetic: 2.85 us -> none  [the longest x1 0.84 us: per_device(): multiplier + observation_weight * (final_state - observations)]
    unnamed x26 -> x14, local copies, waits for them, and re-layouts: 3.82 us -> 1.06 us
    sub x13 -> x0, other arithmetic: 2.49 us -> none  [the longest x9 1.54 us: apply_forward(): east_flow * (west_east[..., 1:] + west_east[..., :-1]) * 0.5]
  transfers between devices with their start and end apart: 38 -> 8, of which waited for: 12 -> 3; matrix products, arithmetic and copies ran while one was open for 2% -> 0% of each run, Pallas kernels for 0% -> 0%
where the time goes in v1:
time: 74.5 us; the launch traced here: 74 us
  starting transfers between devices  42.5 us (57%)
  waiting for transfers between devices  18.6 us (25%)
  Pallas kernels  10.3 us (14%)
  between operations  1.46 us (2%)
  local copies, waits for them, and re-layouts  1.06 us (1%)
    ppermute x8, starting transfers between devices, shifted(): return lax.ppermute(array, axis, pairs)  42.5 us
    ppermute x8, waiting for transfers between devices, shifted(): return lax.ppermute(array, axis, pairs)  18.6 us
    pallas_call x1, Pallas kernels, per_device(): pl.pallas_call(solve_kernel, in_specs=[smem, smem] + vmem(12), out_specs=...  8.26 us
    pallas_call x1, Pallas kernels, per_device(): pl.pallas_call(pack_kernel, in_specs=[smem] + vmem(8), out_specs=vmem(5),...  2.06 us
  transfers between devices with their start and end apart: 8, of which 3 were waited for; matrix products, arithmetic and copies ran while one was open for 0% of the time, Pallas kernels for 0%

profile of v1, /device:TPU:6, one launch (start us, length us, event | category | flops | bytes accessed | tf_op | source)
XLA Modules:
  0.0 74.0 jit_solution(2273262408652618530)
XLA Ops:
  0.6 2.1 %shard_map.148 = (f32[8,16,8,128]{3,2,1,0:T(8,128)}, f32[16,8,128]{2,1,0:T(8,128)}, f32[16,8,128]{2,1,0:T(8,128)}, f32[48,128]{1,0:T(8,128)}, f32[16,128]{1,0:T(8,128)}) custom-call(s32[1]{0:T(128)} %bitcast.1.last_ref, f32[16,8,128]{2,1,0:T(8,128)} %refs_0_.1, f32[16,8,128]{2,1,0:T(8,128)} %refs_1_.1, f32[16,8,128]{2,1,0:T(8,128)} %refs_2_.1, ...), custom_call_target="tpu_custom_call" | custom-call | tf_op jit(solution)/shard_map/pallas_call | solution.py:321
  2.7 7.6 %collective-permute-start.1 = (f32[8,16,8,128]{3,2,1,0:T(8,128)}, f32[8,16,8,128]{3,2,1,0:T(8,128)S(1)}, u32[]{:S(2)}, u32[]{:S(2)}) collective-permute-start(f32[8,16,8,128]{3,2,1,0:T(8,128)} %get-tuple-element.8.own), channel_id=1, source_target_pairs={{1,0},{2,1},{3,2},{4,3},{5,4},{6,5},{7,6},{8,7},{9,8},{10,9},{11,1... | collective-permute-start | bytes 1572872 | tf_op jit(solution)/shard_map/ppermute | solution.py:288
  10.3 1.9 %collective-permute-start = (f32[8,16,8,128]{3,2,1,0:T(8,128)}, f32[8,16,8,128]{3,2,1,0:T(8,128)S(1)}, u32[]{:S(2)}, u32[]{:S(2)}) collective-permute-start(f32[8,16,8,128]{3,2,1,0:T(8,128)} %get-tuple-element.8.own), channel_id=1, source_target_pairs={{0,1},{1,2},{2,3},{3,4},{4,5},{5,6},{6,7},{7,8},{8,9},{9,10},{10,1... | collective-permute-start | bytes 1572872 | tf_op jit(solution)/shard_map/ppermute | solution.py:288
  12.2 3.5 %collective-permute-start.2 = (f32[16,8,128]{2,1,0:T(8,128)}, f32[16,8,128]{2,1,0:T(8,128)S(1)}, u32[]{:S(2)}, u32[]{:S(2)}) collective-permute-start(f32[16,8,128]{2,1,0:T(8,128)} %get-tuple-element.9), channel_id=1, source_target_pairs={{0,32},{32,64},{64,96},{96,128},{128,160},{160,192},{192,224},{224... | collective-permute-start | bytes 196616 | tf_op jit(solution)/shard_map/ppermute | solution.py:288
  15.7 16.8 %collective-permute-start.3 = (f32[16,8,128]{2,1,0:T(8,128)}, f32[16,8,128]{2,1,0:T(8,128)S(1)}, u32[]{:S(2)}, u32[]{:S(2)}) collective-permute-start(f32[16,8,128]{2,1,0:T(8,128)} %get-tuple-element.10), channel_id=1, source_target_pairs={{0,992},{32,0},{64,32},{96,64},{128,96},{160,128},{192,160},{224,1... | collective-permute-start | bytes 196616 | tf_op jit(solution)/shard_map/ppermute | solution.py:288
  32.6 11.2 %collective-permute-done.2.from_west = f32[16,8,128]{2,1,0:T(8,128)S(1)} collective-permute-done((f32[16,8,128]{2,1,0:T(8,128)}, f32[16,8,128]{2,1,0:T(8,128)S(1)}, u32[]{:S(2)}, u32[]{:S(2)}) %collective-permute-start.2) | collective-permute-done | bytes 65568 | tf_op jit(solution)/shard_map/ppermute | solution.py:288
  43.8 0.0 collective-permute-done.3.from_east
  43.8 0.0 copy-start.6
  43.8 0.0 copy-start.5
  43.8 0.0 copy-start.1
  43.8 0.0 copy-start.2
  43.8 2.1 %collective-permute-start.5 = (f32[2,16,8,128]{3,2,1,0:T(8,128)S(1)}, f32[2,16,8,128]{3,2,1,0:T(8,128)S(1)}, u32[]{:S(2)}, u32[]{:S(2)}) collective-permute-start(f32[2,16,8,128]{3,2,1,0:T(8,128)S(1)} %pad_maximum_fusion), channel_id=1, source_target_pairs={{1,0},{2,1},{3,2},{4,3},{5,4},{6,5},{7,6},{8,7},{9,8},{10,9},{11,1... | collective-permute-start | bytes 393224 | tf_op jit(solution)/shard_map/ppermute | solution.py:288
  45.9 2.4 %collective-permute-start.4 = (f32[2,16,8,128]{3,2,1,0:T(8,128)S(1)}, f32[2,16,8,128]{3,2,1,0:T(8,128)S(1)}, u32[]{:S(2)}, u32[]{:S(2)}) collective-permute-start(f32[2,16,8,128]{3,2,1,0:T(8,128)S(1)} %pad_maximum_fusion), channel_id=1, source_target_pairs={{0,1},{1,2},{2,3},{3,4},{4,5},{5,6},{6,7},{7,8},{8,9},{9,10},{10,1... | collective-permute-start | bytes 393224 | tf_op jit(solution)/shard_map/ppermute | solution.py:288
  48.3 0.0 copy-done.6
  48.3 6.3 %collective-permute-start.7 = (f32[16,128]{1,0:T(8,128)S(1)}, f32[16,128]{1,0:T(8,128)S(1)}, u32[]{:S(2)}, u32[]{:S(2)}) collective-permute-start(f32[16,128]{1,0:T(8,128)S(1)} %copy-done.6), channel_id=1, source_target_pairs={{2,0},{3,1},{4,2},{5,3},{6,4},{7,5},{8,6},{9,7},{10,8},{11,9},{12,... | collective-permute-start | bytes 24584 | tf_op jit(solution)/shard_map/ppermute | solution.py:288
  55.3 0.7 collective-permute-done.7.far_north
  56.0 0.0 copy-done.5
  56.0 1.9 %collective-permute-start.6 = (f32[48,128]{1,0:T(8,128)S(1)}, f32[48,128]{1,0:T(8,128)S(1)}, u32[]{:S(2)}, u32[]{:S(2)}) collective-permute-start(f32[48,128]{1,0:T(8,128)S(1)} %copy-done.5), channel_id=1, source_target_pairs={{0,2},{1,3},{2,4},{3,5},{4,6},{5,7},{6,8},{7,9},{8,10},{9,11},{10,... | collective-permute-start | bytes 73736 | tf_op jit(solution)/shard_map/ppermute | solution.py:288
  57.9 0.0 copy-start.3
  57.9 0.0 copy-start.4
  57.9 0.1 fusion.4.cos_ref
  58.0 6.7 %collective-permute-done.6.far_south = f32[48,128]{1,0:T(8,128)S(1)} collective-permute-done((f32[48,128]{1,0:T(8,128)S(1)}, f32[48,128]{1,0:T(8,128)S(1)}, u32[]{:S(2)}, u32[]{:S(2)}) %collective-permute-start.6) | collective-permute-done | bytes 24608 | tf_op jit(solution)/shard_map/ppermute | solution.py:288
  64.7 0.0 collective-permute-done.5.corner_north
  64.7 0.0 collective-permute-done.4.corner_south
  64.7 0.0 collective-permute-done.1.north
  64.7 0.0 collective-permute-done.south
  64.7 0.0 copy-done.1
  64.7 0.0 copy-done.2
  64.7 0.0 copy-done.3
  64.7 0.0 copy-done.4
  64.7 0.0 copy-start
  64.7 1.0 %copy-done = f32[8,16,8,128]{3,2,1,0:T(8,128)S(1)} copy-done((f32[8,16,8,128]{3,2,1,0:T(8,128)S(1)}, f32[8,16,8,128]{3,2,1,0:T(8,128)}, u32[]{:S(2)}) %copy-start) | copy-done | bytes 524312
  65.8 8.3 %shard_map.149 = (f32[16,8,128]{2,1,0:T(8,128)}, f32[16,8,128]{2,1,0:T(8,128)}, f32[16,8,128]{2,1,0:T(8,128)}) custom-call(f32[16]{0:T(128)S(1)} %copy-done.3, f32[16]{0:T(128)S(1)} %copy-done.4, f32[1,256]{1,0:T(1,128)S(1)} %fusion.4.cos_ref, f32[8,16,8,128]{3,2,1,0:T(8,128)S(1)} %copy-done, f32[8,16,8,128]{3,2,1,0:T(8,128)S(1)} %collective-permute-done.south, ...), custom_call_target="tpu_custom_call" | custom-call | tf_op jit(solution)/shard_map/pallas_call | solution.py:354
  (1 shorter events, 0.0 us)
Async XLA Ops:
  2.7 62.0 %collective-permute-start.1 = (f32[8,16,8,128]{3,2,1,0:T(8,128)}, f32[8,16,8,128]{3,2,1,0:T(8,128)S(1)}, u32[]{:S(2)}, u32[]{:S(2)}) collective-permute-start(f32[8,16,8,128]{3,2,1,0:T(8,128)} %get-tuple-element.8.own), channel_id=1, source_target_pairs={{1,0},{2,1},{3,2},{4,3},{5,4},{6,5},{7,6},{8,7},{9,8},{10,9},{11,1... | collective-permute-start | bytes 1572872 | tf_op jit(solution)/shard_map/ppermute | solution.py:288
  10.3 54.4 %collective-permute-start = (f32[8,16,8,128]{3,2,1,0:T(8,128)}, f32[8,16,8,128]{3,2,1,0:T(8,128)S(1)}, u32[]{:S(2)}, u32[]{:S(2)}) collective-permute-start(f32[8,16,8,128]{3,2,1,0:T(8,128)} %get-tuple-element.8.own), channel_id=1, source_target_pairs={{0,1},{1,2},{2,3},{3,4},{4,5},{5,6},{6,7},{7,8},{8,9},{9,10},{10,1... | collective-permute-start | bytes 1572872 | tf_op jit(solution)/shard_map/ppermute | solution.py:288
  12.2 31.6 %collective-permute-start.2 = (f32[16,8,128]{2,1,0:T(8,128)}, f32[16,8,128]{2,1,0:T(8,128)S(1)}, u32[]{:S(2)}, u32[]{:S(2)}) collective-permute-start(f32[16,8,128]{2,1,0:T(8,128)} %get-tuple-element.9), channel_id=1, source_target_pairs={{0,32},{32,64},{64,96},{96,128},{128,160},{160,192},{192,224},{224... | collective-permute-start | bytes 196616 | tf_op jit(solution)/shard_map/ppermute | solution.py:288
  15.7 28.1 %collective-permute-start.3 = (f32[16,8,128]{2,1,0:T(8,128)}, f32[16,8,128]{2,1,0:T(8,128)S(1)}, u32[]{:S(2)}, u32[]{:S(2)}) collective-permute-start(f32[16,8,128]{2,1,0:T(8,128)} %get-tuple-element.10), channel_id=1, source_target_pairs={{0,992},{32,0},{64,32},{96,64},{128,96},{160,128},{192,160},{224,1... | collective-permute-start | bytes 196616 | tf_op jit(solution)/shard_map/ppermute | solution.py:288
  43.8 4.5 %copy-start.6 = (f32[16,128]{1,0:T(8,128)S(1)}, f32[16,128]{1,0:T(8,128)}, u32[]{:S(2)}) copy-start(f32[16,128]{1,0:T(8,128)} %get-tuple-element.12) | copy-start | bytes 24580
  43.8 12.2 %copy-start.5 = (f32[48,128]{1,0:T(8,128)S(1)}, f32[48,128]{1,0:T(8,128)}, u32[]{:S(2)}) copy-start(f32[48,128]{1,0:T(8,128)} %get-tuple-element.11) | copy-start | bytes 73732
  43.8 20.9 %copy-start.1 = (f32[16,8,128]{2,1,0:T(8,128)S(1)}, f32[16,8,128]{2,1,0:T(8,128)}, u32[]{:S(2)}) copy-start(f32[16,8,128]{2,1,0:T(8,128)} %observations.1) | copy-start | bytes 196612
  43.8 20.9 %copy-start.2 = (f32[16,8,128]{2,1,0:T(8,128)S(1)}, f32[16,8,128]{2,1,0:T(8,128)}, u32[]{:S(2)}) copy-start(f32[16,8,128]{2,1,0:T(8,128)} %weight.1) | copy-start | bytes 196612
  43.8 20.8 %collective-permute-start.5 = (f32[2,16,8,128]{3,2,1,0:T(8,128)S(1)}, f32[2,16,8,128]{3,2,1,0:T(8,128)S(1)}, u32[]{:S(2)}, u32[]{:S(2)}) collective-permute-start(f32[2,16,8,128]{3,2,1,0:T(8,128)S(1)} %pad_maximum_fusion), channel_id=1, source_target_pairs={{1,0},{2,1},{3,2},{4,3},{5,4},{6,5},{7,6},{8,7},{9,8},{10,9},{11,1... | collective-permute-start | bytes 393224 | tf_op jit(solution)/shard_map/ppermute | solution.py:288
  45.9 18.8 %collective-permute-start.4 = (f32[2,16,8,128]{3,2,1,0:T(8,128)S(1)}, f32[2,16,8,128]{3,2,1,0:T(8,128)S(1)}, u32[]{:S(2)}, u32[]{:S(2)}) collective-permute-start(f32[2,16,8,128]{3,2,1,0:T(8,128)S(1)} %pad_maximum_fusion), channel_id=1, source_target_pairs={{0,1},{1,2},{2,3},{3,4},{4,5},{5,6},{6,7},{7,8},{8,9},{9,10},{10,1... | collective-permute-start | bytes 393224 | tf_op jit(solution)/shard_map/ppermute | solution.py:288
  48.3 7.7 %collective-permute-start.7 = (f32[16,128]{1,0:T(8,128)S(1)}, f32[16,128]{1,0:T(8,128)S(1)}, u32[]{:S(2)}, u32[]{:S(2)}) collective-permute-start(f32[16,128]{1,0:T(8,128)S(1)} %copy-done.6), channel_id=1, source_target_pairs={{2,0},{3,1},{4,2},{5,3},{6,4},{7,5},{8,6},{9,7},{10,8},{11,9},{12,... | collective-permute-start | bytes 24584 | tf_op jit(solution)/shard_map/ppermute | solution.py:288
  56.0 8.7 %collective-permute-start.6 = (f32[48,128]{1,0:T(8,128)S(1)}, f32[48,128]{1,0:T(8,128)S(1)}, u32[]{:S(2)}, u32[]{:S(2)}) collective-permute-start(f32[48,128]{1,0:T(8,128)S(1)} %copy-done.5), channel_id=1, source_target_pairs={{0,2},{1,3},{2,4},{3,5},{4,6},{5,7},{6,8},{7,9},{8,10},{9,11},{10,... | collective-permute-start | bytes 73736 | tf_op jit(solution)/shard_map/ppermute | solution.py:288
  57.9 6.8 %copy-start.3 = (f32[16]{0:T(128)S(1)}, f32[16]{0:T(128)}, u32[]{:S(2)}) copy-start(f32[16]{0:T(128)} %level_ref.1) | copy-start | bytes 196
  57.9 6.8 %copy-start.4 = (f32[16]{0:T(128)S(1)}, f32[16]{0:T(128)}, u32[]{:S(2)}) copy-start(f32[16]{0:T(128)} %damp_ref.1) | copy-start | bytes 196
  64.7 1.0 %copy-start = (f32[8,16,8,128]{3,2,1,0:T(8,128)S(1)}, f32[8,16,8,128]{3,2,1,0:T(8,128)}, u32[]{:S(2)}) copy-start(f32[8,16,8,128]{3,2,1,0:T(8,128)} %get-tuple-element.8.own) | copy-start | bytes 1572868
